TPU v7x, 32 devices: a whole 2x2x4 slice. The times are simulated.
32 devices in a mesh: samples: 4 (over y, x), features: 4 (over z), rhs: 2 (over core).
Axes of the slice: x: 2, y: 2, z: 4, core: 2. Of those that a mesh axis runs over, the one named last changes fastest.
Arguments:
- design: bfloat16 [32768, 32768], P(('samples', 'rhs'), 'features'), may hold values from -0.03125 to 0.03125
- right_side: float32 [32768, 64], P('features', 'rhs'), may hold values from -6 to 6
- factor: bfloat16 [32768, 768], P('features', 'rhs'), may hold values from -0.03125 to 0.03125
- nystrom_values: float32 [768], replicated, may hold values from 0.5 to 3
Outputs:
- solution: float32 [32768, 64], P('features', 'rhs')
- residual: float32 [32768, 64], P('features', 'rhs')
All inputs are finite; a program needn't handle non-finite values.
Results may differ from a plain program's by a relative error of at most 0.0181.
Values may be sent and summed in bfloat16 or wider, within the bound.
A program may use at most 192 MiB of HBM per device.

v0:
```python
import functools

import jax
import jax.numpy as jnp
from jax import lax
from jax.experimental import pallas as pl
from jax.experimental.pallas import tpu as pltpu
from jax.sharding import PartitionSpec as P

ITERS = 3
MESH = pl.DeviceIdType.MESH
RIDGE = 1.0


def dot_t(left, right):
    return lax.dot_general(
        left,
        right,
        (((1,), (1,)), ((), ())),
        precision=lax.Precision.HIGHEST,
        preferred_element_type=jnp.float32,
    )


def dot_h(left, right):
    return jnp.dot(
        left, right, precision=lax.Precision.HIGHEST, preferred_element_type=jnp.float32
    )


def feature_group(n_rhs):
    me = lax.axis_index("samples") * n_rhs + lax.axis_index("rhs")

    def place(index):
        return {"samples": lax.div(index, n_rhs), "rhs": lax.rem(index, n_rhs)}

    return me, place


def sample_group():
    return lax.axis_index("features"), lambda index: {"features": index}


def others(n, me, body):
    for step in range(1, n):
        body(lax.rem(me + step, n))


def greet(groups):
    barrier = pltpu.get_barrier_semaphore()
    total = 0
    for n, me, place in groups:
        others(
            n,
            me,
            lambda peer: pl.semaphore_signal(
                barrier, inc=1, device_id=place(peer), device_id_type=MESH
            ),
        )
        total += n - 1
    pl.semaphore_wait(barrier, total)


def columns(index, width):
    return pl.ds(pl.multiple_of(index * width, 128), width)


def exchange(n, me, place, source, target, send_sem, recv_sem):
    def copy(step):
        peer = lax.rem(me + step, n)
        return pltpu.make_async_remote_copy(
            src_ref=source(peer),
            dst_ref=target(me),
            send_sem=send_sem.at[step],
            recv_sem=recv_sem.at[step],
            device_id=place(peer),
            device_id_type=MESH,
        )

    copies = [copy(step) for step in range(1, n)]
    for each in copies:
        each.start()
    for each in copies:
        each.wait_recv()
    return copies


def finish(copies):
    for each in copies:
        each.wait_send()


def total_of(own, held, n, me):
    total = own.astype(jnp.float32)
    for step in range(1, n):
        total = total + held[lax.rem(me + step, n)].astype(jnp.float32)
    return total


def images_kernel(n, x_ref, out_ref, held, send_a, recv_a, send_b, recv_b):
    me, place = sample_group()
    width = x_ref.shape[1] // n
    greet([(n, me, place)])
    first = exchange(
        n, me, place,
        lambda peer: x_ref.at[:, columns(peer, width)],
        lambda index: held.at[index],
        send_a, recv_a,
    )
    own = x_ref[:, columns(me, width)]
    out_ref[:, columns(me, width)] = total_of(own, held, n, me).astype(out_ref.dtype)
    second = exchange(
        n, me, place,
        lambda peer: out_ref.at[:, columns(me, width)],
        lambda index: out_ref.at[:, columns(index, width)],
        send_b, recv_b,
    )
    finish(first + second)


def scatter_kernel(n, n_rhs, x_ref, out_ref, held, send_a, recv_a):
    me, place = feature_group(n_rhs)
    width = x_ref.shape[1] // n
    greet([(n, me, place)])
    first = exchange(
        n, me, place,
        lambda peer: x_ref.at[:, columns(peer, width)],
        lambda index: held.at[index],
        send_a, recv_a,
    )
    out_ref[...] = total_of(x_ref[:, columns(me, width)], held, n, me)
    finish(first)


def gather_kernel(n, n_rhs, split, x_ref, out_ref, send_a, recv_a):
    me, place = feature_group(n_rhs)
    rows, wide = out_ref.shape
    width = wide // n

    def part(peer):
        if split:
            return pl.ds(pl.multiple_of(lax.rem(peer, n_rhs) * rows, 16), rows)
        return pl.ds(0, rows)

    greet([(n, me, place)])
    first = exchange(
        n, me, place,
        lambda peer: x_ref.at[part(peer), :],
        lambda index: out_ref.at[:, columns(index, width)],
        send_a, recv_a,
    )
    out_ref[:, columns(me, width)] = x_ref[part(me), :]
    finish(first)


def totals_kernel(
    n, n_rhs, n_feat, x_ref, out_ref, held, across, mine, sa, ra, sb, rb, sc, rc
):
    me, place = feature_group(n_rhs)
    feat, feat_place = sample_group()
    width = x_ref.shape[1] // n
    greet([(n, me, place), (n_feat, feat, feat_place)])
    first = exchange(
        n, me, place,
        lambda peer: x_ref.at[:, columns(peer, width)],
        lambda index: held.at[index],
        sa, ra,
    )
    mine[...] = total_of(x_ref[:, columns(me, width)], held, n, me)
    second = exchange(
        n_feat, feat, feat_place,
        lambda peer: mine,
        lambda index: across.at[index],
        sb, rb,
    )
    across[feat] = mine[...]
    total = across[0]
    for index in range(1, n_feat):
        total = total + across[index]
    out_ref[:, columns(me, width)] = total
    third = exchange(
        n, me, place,
        lambda peer: out_ref.at[:, columns(me, width)],
        lambda index: out_ref.at[:, columns(index, width)],
        sc, rc,
    )
    finish(first + second + third)


def call(kernel, name, ident, shape, dtype, scratch, sems, *args):
    return pl.pallas_call(
        kernel,
        name=name,
        out_shape=jax.ShapeDtypeStruct(shape, dtype),
        in_specs=[pl.BlockSpec(memory_space=pltpu.VMEM)] * len(args),
        out_specs=pl.BlockSpec(memory_space=pltpu.VMEM),
        scratch_shapes=[pltpu.VMEM(s, d) for s, d in scratch]
        + [pltpu.SemaphoreType.DMA((count,)) for count in sems],
        compiler_params=pltpu.CompilerParams(collective_id=ident, has_side_effects=True),
    )(*args)


def shards(n_samp, n_feat, n_rhs, design, right_side, factor, nystrom_values):
    feat_rows, col_share = right_side.shape
    samples = design.shape[0]
    width = col_share * n_rhs
    rank = nystrom_values.shape[0]
    n = n_samp * n_rhs
    piece = feat_rows // n
    samp, rhs = lax.axis_index("samples"), lax.axis_index("rhs")
    shrink = (1.0 + jnp.min(nystrom_values)) / (1.0 + nystrom_values) - 1.0

    def own_rows(block):
        def rows_for(core):
            return lax.dynamic_slice_in_dim(block, (samp * n_rhs + core) * piece, piece, 0)

        parts = [None] * n_rhs
        moved = [rows_for(rhs)]
        for step in range(1, n_rhs):
            pairs = [(i, (i + step) % n_rhs) for i in range(n_rhs)]
            moved.append(lax.ppermute(rows_for((rhs + step) % n_rhs), "rhs", pairs))
        for core in range(n_rhs):
            best = moved[0]
            for step in range(1, n_rhs):
                best = jnp.where((rhs - step) % n_rhs == core, moved[step], best)
            parts[core] = best
        return jnp.concatenate(parts, axis=1)

    images_of = lambda x: call(
        functools.partial(images_kernel, n_feat), "images_sum", 1, x.shape, jnp.bfloat16,
        [((n_feat, width, samples // n_feat), jnp.bfloat16)], [n_feat] * 4, x,
    )
    scatter = lambda x: call(
        functools.partial(scatter_kernel, n, n_rhs), "feature_scatter", 2,
        (width, piece), jnp.float32, [((n, width, piece), jnp.bfloat16)], [n] * 2, x,
    )
    gather = lambda x: call(
        functools.partial(gather_kernel, n, n_rhs, False), "direction_gather", 3,
        (width, feat_rows), x.dtype, [], [n] * 2, x,
    )
    gather_out = lambda x: call(
        functools.partial(gather_kernel, n, n_rhs, True), "output_gather", 4,
        (x.shape[0] // n_rhs, feat_rows), x.dtype, [], [n] * 2, x,
    )

    def totals(x):
        lanes = x.shape[1]
        unit = 128 * n
        padded = -(-lanes // unit) * unit
        x = jnp.pad(x, ((0, 0), (0, padded - lanes)))
        share = (width, padded // n)
        got = call(
            functools.partial(totals_kernel, n, n_rhs, n_feat), "small_totals", 5,
            x.shape, jnp.float32,
            [((n,) + share, jnp.float32), ((n_feat,) + share, jnp.float32), (share, jnp.float32)],
            [n, n, n_feat, n_feat, n, n], x,
        )
        return got[:, :lanes]

    basis = own_rows(factor)
    residual = own_rows(right_side).T

    def parts_of(values):
        upper = values.astype(jnp.bfloat16)
        widened = lax.optimization_barrier(upper).astype(jnp.float32)
        return jnp.concatenate([upper, (values - widened).astype(jnp.bfloat16)], axis=0)

    def factor_inner(values):
        both = jnp.dot(parts_of(values), basis, preferred_element_type=jnp.float32)
        return both[:width] + both[width:]

    def expand(projected):
        both = lax.dot_general(
            parts_of(shrink[None, :] * projected), basis, (((1,), (1,)), ((), ())),
            preferred_element_type=jnp.float32,
        )
        return both[:width] + both[width:]

    projected = totals(factor_inner(residual))
    direction = residual + expand(projected)
    solution = jnp.zeros_like(residual)
    eye = jnp.eye(width, dtype=jnp.float32)
    for iteration in range(ITERS):
        narrow = gather(direction.astype(jnp.bfloat16))
        partial = lax.dot_general(
            narrow, design, (((1,), (1,)), ((), ())), preferred_element_type=jnp.float32
        )
        images = images_of(partial.astype(jnp.bfloat16))
        feature_term = jnp.dot(images, design, preferred_element_type=jnp.float32)
        applied = scatter(feature_term.astype(jnp.bfloat16)) + RIDGE * direction
        last = iteration + 1 == ITERS
        block = dot_t(
            jnp.concatenate([direction, applied], axis=0),
            jnp.concatenate([applied, residual], axis=0),
        )
        small = [block[:width], block[width:]]
        if not last:
            small.append(factor_inner(applied))
        summed = totals(jnp.concatenate(small, axis=1))
        gram = summed[:, :width]
        cross = summed[:, width : 2 * width]
        gram = 0.5 * (gram + gram.T)
        chol_lower = jnp.linalg.cholesky(gram)
        inverse = jax.scipy.linalg.solve_triangular(chol_lower, eye, lower=True)
        back_t = dot_h(dot_h(inverse, cross).T, inverse)
        solution = solution + dot_h(back_t, direction)
        residual = residual - dot_h(back_t, applied)
        if not last:
            image_image = summed[:, 2 * width : 3 * width]
            image_res = summed[:, 3 * width : 4 * width]
            factor_image = summed[:, 4 * width :]
            projected = projected - dot_h(back_t, factor_image)
            scaled = residual + expand(projected)
            image_new = image_res - dot_t(image_image, back_t)
            image_new = image_new + dot_t(factor_image, shrink[None, :] * projected)
            next_t = dot_h(dot_h(inverse, image_new).T, inverse)
            direction = scaled - dot_h(next_t, direction)
    stacked = []
    for core in range(n_rhs):
        rows = slice(core * col_share, (core + 1) * col_share)
        stacked += [solution[rows], residual[rows]]
    whole = gather_out(jnp.concatenate(stacked, axis=0).astype(jnp.bfloat16))
    whole = whole.astype(jnp.float32)
    return whole[:col_share].T, whole[col_share:].T


def solution(mesh):
    placed = (P(("samples", "rhs"), "features"), P("features", "rhs"), P("features", "rhs"), P())
    sizes = (mesh.shape["samples"], mesh.shape["features"], mesh.shape["rhs"])
    return jax.shard_map(
        functools.partial(shards, *sizes),
        mesh=mesh,
        in_specs=placed,
        out_specs=(P("features", "rhs"), P("features", "rhs")),
        check_vma=False,
    )
```

profile of v0, /device:TPU:1, one launch (start us, length us, event | category | flops | bytes accessed | tf_op | source)
XLA Modules:
  0.0 521.0 jit_solution(17878659787915153946)
XLA Ops:
  9.9 19.8 %small_totals.4 = f32[64,1024]{1,0:T(8,128)} custom-call(f32[64,1024]{1,0:T(8,128)} %pad.8.x_ref), custom_call_target="tpu_custom_call" | custom-call | tf_op jit(solution)/shard_map/small_totals/pallas_call | solution.py:191
  33.0 16.8 %direction_gather.3 = bf16[64,8192]{1,0:T(8,128)(2,1)} custom-call(bf16[64,1024]{1,0:T(8,128)(2,1)} %get-tuple-element.8.x_ref), custom_call_target="tpu_custom_call" | custom-call | tf_op jit(solution)/shard_map/direction_gather/pallas_call | solution.py:191
  49.8 28.2 %convolution_convert_fusion.5.x_ref = bf16[64,4096]{1,0:T(8,128)(2,1)} fusion(bf16[64,8192]{1,0:T(8,128)(2,1)} %direction_gather.3, bf16[4096,8192]{1,0:T(8,128)(2,1)} %param.7), kind=kOutput, calls=%fused_computation.5 | convolution fusion | flops 4295229440 | bytes 68681728 | tf_op jit(solution)/shard_map/dot_general | solution.py:285
  78.1 25.1 %images_sum.3 = bf16[64,4096]{1,0:T(8,128)(2,1)} custom-call(bf16[64,4096]{1,0:T(8,128)(2,1)} %convolution_convert_fusion.5.x_ref), custom_call_target="tpu_custom_call" | custom-call | tf_op jit(solution)/shard_map/images_sum/pallas_call | solution.py:191
  103.2 25.6 %convolution_convert_fusion.2.x_ref = bf16[64,8192]{1,0:T(8,128)(2,1)} fusion(bf16[64,4096]{1,0:T(8,128)(2,1)} %images_sum.3, bf16[4096,8192]{1,0:T(8,128)(2,1)} %param.7), kind=kOutput, calls=%fused_computation.2 | convolution fusion | flops 4295491584 | bytes 68681728 | tf_op jit(solution)/shard_map/dot_general | solution.py:289
  128.7 16.8 %feature_scatter.3 = f32[64,1024]{1,0:T(8,128)} custom-call(bf16[64,8192]{1,0:T(8,128)(2,1)} %convolution_convert_fusion.2.x_ref), custom_call_target="tpu_custom_call" | custom-call | tf_op jit(solution)/shard_map/feature_scatter/pallas_call | solution.py:191
  148.3 20.7 %small_totals.5 = f32[64,1024]{1,0:T(8,128)} custom-call(f32[64,1024]{1,0:T(8,128)} %pad_maximum_fusion.1.x_ref), custom_call_target="tpu_custom_call" | custom-call | tf_op jit(solution)/shard_map/small_totals/pallas_call | solution.py:191
  170.7 5.8 %cholesky.59 = f32[64,64]{1,0:T(8,128)S(1)} custom-call(f32[64,64]{1,0:T(8,128)S(1)} %fusion.77), custom_call_target="Cholesky" | custom-call | tf_op jit(solution)/shard_map/jit(cholesky)/cholesky | solution.py:303
  190.3 16.6 %direction_gather.4 = bf16[64,8192]{1,0:T(8,128)(2,1)} custom-call(bf16[64,1024]{1,0:T(8,128)(2,1)} %get-tuple-element.28.x_ref), custom_call_target="tpu_custom_call" | custom-call | tf_op jit(solution)/shard_map/direction_gather/pallas_call | solution.py:191
  206.9 28.4 %convolution_convert_fusion.4.x_ref = bf16[64,4096]{1,0:T(8,128)(2,1)} fusion(bf16[64,8192]{1,0:T(8,128)(2,1)} %direction_gather.4, bf16[4096,8192]{1,0:T(8,128)(2,1)} %param.7), kind=kOutput, calls=%fused_computation.4 | convolution fusion | flops 4295229440 | bytes 68681728 | tf_op jit(solution)/shard_map/dot_general | solution.py:285
  235.3 25.4 %images_sum.4 = bf16[64,4096]{1,0:T(8,128)(2,1)} custom-call(bf16[64,4096]{1,0:T(8,128)(2,1)} %convolution_convert_fusion.4.x_ref), custom_call_target="tpu_custom_call" | custom-call | tf_op jit(solution)/shard_map/images_sum/pallas_call | solution.py:191
  260.7 25.6 %convolution_convert_fusion.1.x_ref = bf16[64,8192]{1,0:T(8,128)(2,1)} fusion(bf16[64,4096]{1,0:T(8,128)(2,1)} %images_sum.4, bf16[4096,8192]{1,0:T(8,128)(2,1)} %param.7), kind=kOutput, calls=%fused_computation.1 | convolution fusion | flops 4295491584 | bytes 68681728 | tf_op jit(solution)/shard_map/dot_general | solution.py:289
  286.3 16.4 %feature_scatter.4 = f32[64,1024]{1,0:T(8,128)} custom-call(bf16[64,8192]{1,0:T(8,128)(2,1)} %convolution_convert_fusion.1.x_ref), custom_call_target="tpu_custom_call" | custom-call | tf_op jit(solution)/shard_map/feature_scatter/pallas_call | solution.py:191
  305.5 20.9 %small_totals.6 = f32[64,1024]{1,0:T(8,128)} custom-call(f32[64,1024]{1,0:T(8,128)} %pad_maximum_fusion.2.x_ref), custom_call_target="tpu_custom_call" | custom-call | tf_op jit(solution)/shard_map/small_totals/pallas_call | solution.py:191
  328.1 5.8 %cholesky.70 = f32[64,64]{1,0:T(8,128)S(1)} custom-call(f32[64,64]{1,0:T(8,128)S(1)} %fusion.74), custom_call_target="Cholesky" | custom-call | tf_op jit(solution)/shard_map/jit(cholesky)/cholesky | solution.py:303
  348.1 16.7 %direction_gather.5 = bf16[64,8192]{1,0:T(8,128)(2,1)} custom-call(bf16[64,1024]{1,0:T(8,128)(2,1)} %get-tuple-element.32.x_ref), custom_call_target="tpu_custom_call" | custom-call | tf_op jit(solution)/shard_map/direction_gather/pallas_call | solution.py:191
  364.7 28.5 %convolution_convert_fusion.3.x_ref = bf16[64,4096]{1,0:T(8,128)(2,1)} fusion(bf16[64,8192]{1,0:T(8,128)(2,1)} %direction_gather.5, bf16[4096,8192]{1,0:T(8,128)(2,1)} %param.7), kind=kOutput, calls=%fused_computation.3 | convolution fusion | flops 4295229440 | bytes 68681728 | tf_op jit(solution)/shard_map/dot_general | solution.py:285
  393.2 25.3 %images_sum.5 = bf16[64,4096]{1,0:T(8,128)(2,1)} custom-call(bf16[64,4096]{1,0:T(8,128)(2,1)} %convolution_convert_fusion.3.x_ref), custom_call_target="tpu_custom_call" | custom-call | tf_op jit(solution)/shard_map/images_sum/pallas_call | solution.py:191
  418.5 25.6 %convolution_convert_fusion.x_ref = bf16[64,8192]{1,0:T(8,128)(2,1)} fusion(bf16[64,4096]{1,0:T(8,128)(2,1)} %images_sum.5, bf16[4096,8192]{1,0:T(8,128)(2,1)} %param.7), kind=kOutput, calls=%fused_computation | convolution fusion | flops 4295491584 | bytes 68681728 | tf_op jit(solution)/shard_map/dot_general | solution.py:289
  444.1 17.0 %feature_scatter.5 = f32[64,1024]{1,0:T(8,128)} custom-call(bf16[64,8192]{1,0:T(8,128)(2,1)} %convolution_convert_fusion.x_ref), custom_call_target="tpu_custom_call" | custom-call | tf_op jit(solution)/shard_map/feature_scatter/pallas_call | solution.py:191
  463.4 21.1 %small_totals.7 = f32[64,1024]{1,0:T(8,128)} custom-call(f32[64,1024]{1,0:T(8,128)} %select_maximum_fusion.x_ref), custom_call_target="tpu_custom_call" | custom-call | tf_op jit(solution)/shard_map/small_totals/pallas_call | solution.py:191
  486.3 5.8 %cholesky.81 = f32[64,64]{1,0:T(8,128)S(1)} custom-call(f32[64,64]{1,0:T(8,128)S(1)} %fusion.71), custom_call_target="Cholesky" | custom-call | tf_op jit(solution)/shard_map/jit(cholesky)/cholesky | solution.py:303
  493.5 4.9 custom-call.9
  501.7 16.4 %output_gather.1 = bf16[64,8192]{1,0:T(8,128)(2,1)} custom-call(bf16[128,1024]{1,0:T(8,128)(2,1)} %pad_maximum_fusion.3.x_ref), custom_call_target="tpu_custom_call" | custom-call | tf_op jit(solution)/shard_map/output_gather/pallas_call | solution.py:191
  (101 shorter events, 59.8 us)
Async XLA Ops:
  1.9 5.2 %collective-permute-start.1 = (bf16[1024,384]{1,0:T(8,128)(2,1)S(1)}, bf16[1024,384]{1,0:T(8,128)(2,1)}, u32[]{:S(2)}, u32[]{:S(2)}) collective-permute-start(bf16[1024,384]{1,0:T(8,128)(2,1)S(1)} %constant_dynamic-slice_fusion), channel_id=1, source_target_pairs={{0,1},{1,0},{2,3},{3,2},{4,5},{5,4},{6,7},{7,6},{8,9},{9,8},{10,11... | collective-permute-start | bytes 2359304 | tf_op jit(solution)/shard_map/ppermute | solution.py:221
  2.9 3.2 collective-permute-start
  147.1 37.1 %copy-start = (f32[64,1024]{1,0:T(8,128)S(1)}, f32[64,1024]{1,0:T(8,128)}, u32[]{:S(2)}) copy-start(f32[64,1024]{1,0:T(8,128)} %small_totals.4) | copy-start | bytes 786436
where the time goes:
time: 523 us; the launch traced here: 521 us
  Pallas kernels  275 us (53%)
  matrix products  183 us (35%)
  other arithmetic  53.2 us (10%)
  local copies, waits for them, and re-layouts  7.11 us (1%)
    pallas_call x14, Pallas kernels, call(): pl.pallas_call(kernel, name=name, out_shape=jax.ShapeDtypeStruct(shape, d...  275 us
    dot_general x3, matrix products, shards(): lax.dot_general(narrow, design, (((1,), (1,)), ((), ())), preferred_eleme...  85.1 us
    dot_general x3, matrix products, shards(): feature_term = jnp.dot(images, design, preferred_element_type=jnp.float32)  76.7 us
    another operation x9, other arithmetic, shards(): chol_lower = jnp.linalg.cholesky(gram)  19.6 us
    another operation x6, other arithmetic, shards(): inverse = jax.scipy.linalg.solve_triangular(chol_lower, eye, lower=True)  16.6 us
    dot_general x20, matrix products, dot_h(): jnp.dot(left, right, precision=lax.Precision.HIGHEST, preferred_element_t...  11.2 us
  transfers between devices with their start and end apart: 2, of which 0 were waited for; matrix products, arithmetic and copies ran while one was open for 1% of the time, Pallas kernels for 0%

commit v1 on v0

--- a/solution.py
+++ b/solution.py
@@ -10,6 +10,8 @@
 ITERS = 3
 MESH = pl.DeviceIdType.MESH
 RIDGE = 1.0
+EARLY = 2
+LATE = 2
 
 
 def dot_t(left, right):
@@ -97,39 +99,355 @@
     return total
 
 
-def images_kernel(n, x_ref, out_ref, held, send_a, recv_a, send_b, recv_b):
-    me, place = sample_group()
-    width = x_ref.shape[1] // n
-    greet([(n, me, place)])
-    first = exchange(
-        n, me, place,
-        lambda peer: x_ref.at[:, columns(peer, width)],
-        lambda index: held.at[index],
-        send_a, recv_a,
-    )
-    own = x_ref[:, columns(me, width)]
-    out_ref[:, columns(me, width)] = total_of(own, held, n, me).astype(out_ref.dtype)
-    second = exchange(
-        n, me, place,
-        lambda peer: out_ref.at[:, columns(me, width)],
-        lambda index: out_ref.at[:, columns(index, width)],
-        send_b, recv_b,
-    )
-    finish(first + second)
-
-
-def scatter_kernel(n, n_rhs, x_ref, out_ref, held, send_a, recv_a):
-    me, place = feature_group(n_rhs)
-    width = x_ref.shape[1] // n
-    greet([(n, me, place)])
-    first = exchange(
-        n, me, place,
-        lambda peer: x_ref.at[:, columns(peer, width)],
-        lambda index: held.at[index],
-        send_a, recv_a,
-    )
-    out_ref[...] = total_of(x_ref[:, columns(me, width)], held, n, me)
-    finish(first)
+def other_index(me, step, n):
+    if n & (n - 1):
+        return None
+    bit, total = 1, 0
+    while bit < n:
+        total = total + ((me // bit + step // bit) % 2) * bit
+        bit *= 2
+    return total
+
+
+def operator_kernel(
+    n_samp, n_rhs, n_feat, early, late,
+    x_ref, design, out_ref,
+    slots, narrow, acc, part, up, cross, images, give, side, side_in, chip, chip_in, own,
+    load_sem, piece_send, piece_recv, twin_send, twin_recv,
+    up_send, up_recv, cross_recv, down_send, down_recv,
+    side_send, side_recv, chip_send, chip_recv,
+):
+    samp, core = lax.axis_index("samples"), lax.axis_index("rhs")
+    feat = lax.axis_index("features")
+    n = n_samp * n_rhs
+    count, width, chunk = part.shape
+    held = slots.shape[0]
+    piece = x_ref.shape[1]
+    half = n_feat // 2
+    low = feat < half
+    inner = jnp.logical_or(feat == half - 1, feat == half)
+    outer = jnp.logical_not(inner)
+    first_end, last_end = feat == 0, feat == n_feat - 1
+    is_end = jnp.logical_or(first_end, last_end)
+    has_prev = jnp.logical_not(is_end)
+    following = jnp.where(low, feat + 1, feat - 1)
+    before = jnp.where(low, feat - 1, feat + 1)
+
+    def chip_of(step):
+        return other_index(samp, step, n_samp)
+
+    def core_of(step):
+        return other_index(core, step, n_rhs)
+
+    def cols(chip_index, core_index):
+        return columns(chip_index * n_rhs + core_index, piece)
+
+    def load(c):
+        return pltpu.make_async_copy(
+            design.at[pl.ds(pl.multiple_of(c * chunk, chunk), chunk), :],
+            slots.at[lax.rem(c, held)],
+            load_sem.at[lax.rem(c, held)],
+        )
+
+    def remote(src, dst, send, recv, where):
+        return pltpu.make_async_remote_copy(
+            src_ref=src, dst_ref=dst, send_sem=send, recv_sem=recv,
+            device_id=where, device_id_type=MESH,
+        )
+
+    def loop(low_bound, high_bound, body):
+        def step(i, carry):
+            body(i)
+            return carry
+
+        lax.fori_loop(low_bound, high_bound, step, 0)
+
+    loop(0, held, lambda c: load(c).start())
+
+    barrier = pltpu.get_barrier_semaphore()
+
+    def signal(where):
+        pl.semaphore_signal(barrier, inc=1, device_id=where, device_id_type=MESH)
+
+    for step in range(1, n_samp):
+        signal({"samples": chip_of(step)})
+    for step in range(1, n_rhs):
+        signal({"rhs": core_of(step)})
+
+    @pl.when(jnp.logical_not(first_end))
+    def _():
+        signal({"features": feat - 1})
+
+    @pl.when(jnp.logical_not(last_end))
+    def _():
+        signal({"features": feat + 1})
+
+    greeted = n_samp - 1 + n_rhs - 1
+    pl.semaphore_wait(
+        barrier, jnp.where(is_end, greeted + 1, greeted + 2) if n_feat > 1 else greeted
+    )
+
+    def piece_copy(step):
+        return remote(
+            x_ref, narrow.at[:, cols(samp, core)], piece_send.at[step], piece_recv.at[step],
+            {"samples": chip_of(step)},
+        )
+
+    def twin_copy(step, other):
+        held_piece = narrow.at[:, cols(chip_of(step), core)]
+        return remote(
+            held_piece, held_piece, twin_send.at[step, other], twin_recv.at[step, other],
+            {"rhs": core_of(other)},
+        )
+
+    for step in range(1, n_samp):
+        piece_copy(step).start()
+    narrow[:, cols(samp, core)] = x_ref[...]
+
+    def first_terms(place_cols, fresh):
+        for c in range(early):
+            term = lax.dot_general(
+                narrow[:, place_cols], slots[c, :, place_cols],
+                (((1,), (1,)), ((), ())), preferred_element_type=jnp.float32,
+            )
+            part[c] = part[c] + term
+
+    for c in range(early):
+        part[c] = jnp.zeros((width, chunk), jnp.float32)
+    acc[...] = jnp.zeros_like(acc)
+    for c in range(early):
+        load(c).wait()
+
+    def arrive(step):
+        @pl.when(step > 0)
+        def _():
+            piece_copy(step).wait_recv()
+
+        for other in range(1, n_rhs):
+            twin_copy(step, other).start()
+
+        def by_core(other):
+            @pl.when(other > 0)
+            def _():
+                twin_copy(step, other).wait_recv()
+
+            first_terms(cols(chip_of(step), core_of(other)), False)
+
+        loop(0, n_rhs, by_core)
+
+    loop(0, n_samp, arrive)
+
+    def up_copy(c):
+        return remote(
+            give.at[c], up.at[c], up_send.at[c], up_recv.at[c], {"features": following}
+        )
+
+    def cross_copy(c):
+        return remote(
+            give.at[c], cross.at[c], up_send.at[c], cross_recv.at[c], {"features": following}
+        )
+
+    def down_copy(c):
+        return remote(
+            images.at[c], images.at[c], down_send.at[c], down_recv.at[c], {"features": before}
+        )
+
+    def pass_up(c):
+        @pl.when(inner)
+        def _():
+            cross_copy(c).start()
+
+        @pl.when(outer)
+        def _():
+            up_copy(c).start()
+
+    def up_first(c):
+        @pl.when(is_end)
+        def _():
+            give[c] = part[c].astype(give.dtype)
+            pass_up(c)
+
+    def up_step(c):
+        @pl.when(has_prev)
+        def _():
+            up_copy(c).wait_recv()
+            total = part[c] + up[c].astype(jnp.float32)
+            part[c] = total
+            give[c] = total.astype(give.dtype)
+            pass_up(c)
+
+    def cross_step(c):
+        @pl.when(inner)
+        def _():
+            cross_copy(c).wait_recv()
+            images[c] = (part[c] + cross[c].astype(jnp.float32)).astype(images.dtype)
+
+            @pl.when(has_prev)
+            def _():
+                down_copy(c).start()
+
+    def ready(c):
+        @pl.when(outer)
+        def _():
+            down_copy(c).wait_recv()
+
+            @pl.when(has_prev)
+            def _():
+                down_copy(c).start()
+
+    def image_step(c):
+        load(c).wait()
+        part[c] = lax.dot_general(
+            narrow[...], slots[lax.rem(c, held)],
+            (((1,), (1,)), ((), ())), preferred_element_type=jnp.float32,
+        )
+        up_first(c)
+        loop(jnp.where(c == early, 0, c - 1), c, up_step)
+        loop(jnp.where(c == early + 1, 0, jnp.where(c == early, 0, c - 2)),
+             jnp.where(c == early, 0, c - 1), cross_step)
+
+    def feature_step(c):
+        ready(c)
+        acc[...] = acc[...] + jnp.dot(
+            images[c], slots[lax.rem(c, held)], preferred_element_type=jnp.float32
+        )
+
+        @pl.when(c + held < count)
+        def _():
+            load(c + held).start()
+
+    for c in range(early):
+        up_first(c)
+
+    spare = count - held
+    middle = spare + max((held - late) // 2 - 1, 0)
+
+    def both_steps(turn):
+        loop(jnp.where(turn == 0, early, held), jnp.where(turn == 0, held, count), image_step)
+
+        def step(c):
+            feature_step(c)
+
+            @pl.when(jnp.logical_and(turn == 1, c == middle))
+            def _():
+                up_step(count - 1)
+                cross_step(count - 2)
+
+        loop(jnp.where(turn == 0, 0, spare), jnp.where(turn == 0, spare, count - late), step)
+
+    loop(0, 2, both_steps)
+    cross_step(count - 1)
+    for c in range(count - late, count):
+        ready(c)
+
+    def piece_total(place_cols):
+        total = acc[:, place_cols]
+        for c in range(count - late, count):
+            total = total + jnp.dot(
+                images[c], slots[c % held, :, place_cols], preferred_element_type=jnp.float32
+            )
+        return total
+
+    def side_copy(step, other):
+        return remote(
+            side.at[step, other], side_in.at[step, other],
+            side_send.at[step, other], side_recv.at[step, other], {"rhs": core_of(other)},
+        )
+
+    def chip_copy(step):
+        return remote(
+            chip.at[step], chip_in.at[step], chip_send.at[step], chip_recv.at[step],
+            {"samples": chip_of(step)},
+        )
+
+    def chip_total(step):
+        total = own[...]
+        for other in range(1, n_rhs):
+            side_copy(step, other).wait_recv()
+            total = total + side_in[step, other].astype(jnp.float32)
+        return total
+
+    def leave(i):
+        step = n_samp - 1 - i
+
+        def by_core(j):
+            other = n_rhs - 1 - j
+            total = piece_total(cols(chip_of(step), core_of(other)))
+
+            @pl.when(other > 0)
+            def _():
+                side[step, other] = total.astype(side.dtype)
+                side_copy(step, other).start()
+
+            @pl.when(jnp.logical_and(other == min(1, n_rhs - 1), step < n_samp - 1))
+            def _():
+                chip[step + 1] = chip_total(step + 1).astype(chip.dtype)
+                chip_copy(step + 1).start()
+
+            @pl.when(other == 0)
+            def _():
+                own[...] = total
+
+        loop(0, n_rhs, by_core)
+
+    loop(0, n_samp, leave)
+    out = chip_total(0)
+    for step in range(n_samp - 1, 0, -1):
+        chip_copy(step).wait_recv()
+        out = out + chip_in[step].astype(jnp.float32)
+    out_ref[...] = out
+
+    for step in range(1, n_samp):
+        piece_copy(step).wait_send()
+        chip_copy(step).wait_send()
+
+    def end_core(step):
+        for other in range(1, n_rhs):
+            twin_copy(step, other).wait_send()
+            side_copy(step, other).wait_send()
+
+    loop(0, n_samp, end_core)
+
+    def end_chunk(c):
+        up_copy(c).wait_send()
+
+        @pl.when(has_prev)
+        def _():
+            down_copy(c).wait_send()
+
+    loop(0, count, end_chunk)
+
+
+def apply_operator(n_samp, n_rhs, n_feat, x, design):
+    width, piece = x.shape
+    rows, feats = design.shape
+    chunk = min(512, rows // 4)
+    count = rows // chunk
+    held = min(count, (48 << 20) // (chunk * feats * 2))
+    wide = (width, piece)
+    blocks = (count, width, chunk)
+    vmem, dma = pltpu.VMEM, pltpu.SemaphoreType.DMA
+    bf16, f32 = jnp.bfloat16, jnp.float32
+    return pl.pallas_call(
+        functools.partial(operator_kernel, n_samp, n_rhs, n_feat, EARLY, LATE),
+        name="operator",
+        out_shape=jax.ShapeDtypeStruct(wide, f32),
+        in_specs=[pl.BlockSpec(memory_space=vmem), pl.BlockSpec(memory_space=pl.ANY)],
+        out_specs=pl.BlockSpec(memory_space=vmem),
+        scratch_shapes=[
+            vmem((held, chunk, feats), bf16), vmem((width, feats), bf16), vmem((width, feats), f32),
+            vmem(blocks, f32), vmem(blocks, bf16), vmem(blocks, bf16), vmem(blocks, bf16),
+            vmem(blocks, bf16),
+            vmem((n_samp, n_rhs) + wide, bf16), vmem((n_samp, n_rhs) + wide, bf16),
+            vmem((n_samp,) + wide, bf16), vmem((n_samp,) + wide, bf16), vmem(wide, f32),
+            dma((held,)), dma((n_samp,)), dma((n_samp,)), dma((n_samp, n_rhs)), dma((n_samp, n_rhs)),
+            dma((count,)), dma((count,)), dma((count,)), dma((count,)), dma((count,)),
+            dma((n_samp, n_rhs)), dma((n_samp, n_rhs)), dma((n_samp,)), dma((n_samp,)),
+        ],
+        compiler_params=pltpu.CompilerParams(
+            collective_id=1, has_side_effects=True, vmem_limit_bytes=60 << 20
+        ),
+    )(x, design)
 
 
 def gather_kernel(n, n_rhs, split, x_ref, out_ref, send_a, recv_a):
@@ -226,18 +544,6 @@
             parts[core] = best
         return jnp.concatenate(parts, axis=1)
 
-    images_of = lambda x: call(
-        functools.partial(images_kernel, n_feat), "images_sum", 1, x.shape, jnp.bfloat16,
-        [((n_feat, width, samples // n_feat), jnp.bfloat16)], [n_feat] * 4, x,
-    )
-    scatter = lambda x: call(
-        functools.partial(scatter_kernel, n, n_rhs), "feature_scatter", 2,
-        (width, piece), jnp.float32, [((n, width, piece), jnp.bfloat16)], [n] * 2, x,
-    )
-    gather = lambda x: call(
-        functools.partial(gather_kernel, n, n_rhs, False), "direction_gather", 3,
-        (width, feat_rows), x.dtype, [], [n] * 2, x,
-    )
     gather_out = lambda x: call(
         functools.partial(gather_kernel, n, n_rhs, True), "output_gather", 4,
         (x.shape[0] // n_rhs, feat_rows), x.dtype, [], [n] * 2, x,
@@ -281,13 +587,10 @@
     solution = jnp.zeros_like(residual)
     eye = jnp.eye(width, dtype=jnp.float32)
     for iteration in range(ITERS):
-        narrow = gather(direction.astype(jnp.bfloat16))
-        partial = lax.dot_general(
-            narrow, design, (((1,), (1,)), ((), ())), preferred_element_type=jnp.float32
-        )
-        images = images_of(partial.astype(jnp.bfloat16))
-        feature_term = jnp.dot(images, design, preferred_element_type=jnp.float32)
-        applied = scatter(feature_term.astype(jnp.bfloat16)) + RIDGE * direction
+        summed_features = apply_operator(
+            n_samp, n_rhs, n_feat, direction.astype(jnp.bfloat16), design
+        )
+        applied = summed_features + RIDGE * direction
         last = iteration + 1 == ITERS
         block = dot_t(
             jnp.concatenate([direction, applied], axis=0),

time: 523 us -> 353 us (0.67)
  matrix products: 183 us -> 17.7 us
    pallas_call x14 -> x5, Pallas kernels: 275 us -> 85.5 us  [call(): pl.pallas_call(kernel, name=name, out_shape=jax.ShapeDtypeStruct(shape, d...]
    pallas_call x0 -> x3, Pallas kernels: none -> 185 us  [apply_operator(): pl.pallas_call(functools.partial(operator_kernel, n_samp, n_rhs, n_feat,...]
    dot_general x6 -> x0, matrix products: 162 us -> none  [the longest x3 85.1 us: shards(): lax.dot_general(narrow, design, (((1,), (1,)), ((), ())), preferred_eleme...]
where the time goes in v1:
time: 353 us; the launch traced here: 351 us
  Pallas kernels  270 us (76%)
  other arithmetic  53.2 us (15%)
  matrix products  17.7 us (5%)
  local copies, waits for them, and re-layouts  7.25 us (2%)
    pallas_call x3, Pallas kernels, apply_operator(): pl.pallas_call(functools.partial(operator_kernel, n_samp, n_rhs, n_feat,...  185 us
    pallas_call x5, Pallas kernels, call(): pl.pallas_call(kernel, name=name, out_shape=jax.ShapeDtypeStruct(shape, d...  85.5 us
    another operation x9, other arithmetic, shards(): chol_lower = jnp.linalg.cholesky(gram)  19.6 us
    another operation x6, other arithmetic, shards(): inverse = jax.scipy.linalg.solve_triangular(chol_lower, eye, lower=True)  16.6 us
    dot_general x20, matrix products, dot_h(): jnp.dot(left, right, precision=lax.Precision.HIGHEST, preferred_element_t...  11.2 us
  transfers between devices with their start and end apart: 2, of which 0 were waited for; matrix products, arithmetic and copies ran while one was open for 1% of the time, Pallas kernels for 0%

profile of v1, /device:TPU:1, one launch (start us, length us, event | category | flops | bytes accessed | tf_op | source)
XLA Modules:
  0.0 351.2 jit_solution(14102677452398428884)
XLA Ops:
  1.7 1.2 constant_dynamic-slice_fusion
  3.4 1.3 reduce_min.9
  7.1 1.7 broadcast_select_fusion.1
  9.9 19.7 %small_totals.4 = f32[64,1024]{1,0:T(8,128)} custom-call(f32[64,1024]{1,0:T(8,128)} %pad.8.x_ref), custom_call_target="tpu_custom_call" | custom-call | tf_op jit(solution)/shard_map/small_totals/pallas_call | solution.py:509
  32.9 61.7 %operator.3 = f32[64,1024]{1,0:T(8,128)} custom-call(bf16[64,1024]{1,0:T(8,128)(2,1)} %get-tuple-element.8.x_ref, bf16[4096,8192]{1,0:T(8,128)(2,1)} %design.5), custom_call_target="tpu_custom_call" | custom-call | tf_op jit(solution)/shard_map/operator/pallas_call | solution.py:431
  97.4 16.5 %small_totals.5 = f32[64,1024]{1,0:T(8,128)} custom-call(f32[64,1024]{1,0:T(8,128)} %pad_maximum_fusion.1.x_ref), custom_call_target="tpu_custom_call" | custom-call | tf_op jit(solution)/shard_map/small_totals/pallas_call | solution.py:509
  115.8 5.8 %cholesky.59 = f32[64,64]{1,0:T(8,128)S(1)} custom-call(f32[64,64]{1,0:T(8,128)S(1)} %fusion.77), custom_call_target="Cholesky" | custom-call | tf_op jit(solution)/shard_map/jit(cholesky)/cholesky | solution.py:606
  123.0 4.9 %custom-call.7 = f32[1,64,64]{1,2,0:T(8,128)S(1)} custom-call(f32[1,64,64]{2,1,0:T(8,128)S(1)} %fusion.67), custom_call_target="InvertDiagBlocksLowerTriangular" | custom-call | tf_op jit(solution)/shard_map/jit(_solve_triangular)/triangular_solve | solution.py:607
  128.1 1.0 fusion.85
  129.7 1.2 multiply_convert_fusion.1
  133.0 1.0 fusion.106
  134.0 61.7 %operator.4 = f32[64,1024]{1,0:T(8,128)} custom-call(bf16[64,1024]{1,0:T(8,128)(2,1)} %get-tuple-element.28.x_ref, bf16[4096,8192]{1,0:T(8,128)(2,1)} %design.5), custom_call_target="tpu_custom_call" | custom-call | tf_op jit(solution)/shard_map/operator/pallas_call | solution.py:431
  198.5 16.1 %small_totals.6 = f32[64,1024]{1,0:T(8,128)} custom-call(f32[64,1024]{1,0:T(8,128)} %pad_maximum_fusion.2.x_ref), custom_call_target="tpu_custom_call" | custom-call | tf_op jit(solution)/shard_map/small_totals/pallas_call | solution.py:509
  216.4 5.8 %cholesky.70 = f32[64,64]{1,0:T(8,128)S(1)} custom-call(f32[64,64]{1,0:T(8,128)S(1)} %fusion.74), custom_call_target="Cholesky" | custom-call | tf_op jit(solution)/shard_map/jit(cholesky)/cholesky | solution.py:606
  223.6 4.9 %custom-call.8 = f32[1,64,64]{1,2,0:T(8,128)S(1)} custom-call(f32[1,64,64]{2,1,0:T(8,128)S(1)} %fusion.68), custom_call_target="InvertDiagBlocksLowerTriangular" | custom-call | tf_op jit(solution)/shard_map/jit(_solve_triangular)/triangular_solve | solution.py:607
  230.4 1.2 fusion.107
  233.6 1.0 fusion.108
  234.7 61.6 %operator.5 = f32[64,1024]{1,0:T(8,128)} custom-call(bf16[64,1024]{1,0:T(8,128)(2,1)} %get-tuple-element.32.x_ref, bf16[4096,8192]{1,0:T(8,128)(2,1)} %design.5), custom_call_target="tpu_custom_call" | custom-call | tf_op jit(solution)/shard_map/operator/pallas_call | solution.py:431
  298.5 16.8 %small_totals.7 = f32[64,1024]{1,0:T(8,128)} custom-call(f32[64,1024]{1,0:T(8,128)} %select_maximum_fusion.x_ref), custom_call_target="tpu_custom_call" | custom-call | tf_op jit(solution)/shard_map/small_totals/pallas_call | solution.py:509
  317.0 5.8 %cholesky.81 = f32[64,64]{1,0:T(8,128)S(1)} custom-call(f32[64,64]{1,0:T(8,128)S(1)} %fusion.71), custom_call_target="Cholesky" | custom-call | tf_op jit(solution)/shard_map/jit(cholesky)/cholesky | solution.py:606
  324.2 4.9 %custom-call.9 = f32[1,64,64]{1,2,0:T(8,128)S(1)} custom-call(f32[1,64,64]{2,1,0:T(8,128)S(1)} %fusion.69), custom_call_target="InvertDiagBlocksLowerTriangular" | custom-call | tf_op jit(solution)/shard_map/jit(_solve_triangular)/triangular_solve | solution.py:607
  332.1 16.2 %output_gather.1 = bf16[64,8192]{1,0:T(8,128)(2,1)} custom-call(bf16[128,1024]{1,0:T(8,128)(2,1)} %pad_maximum_fusion.3.x_ref), custom_call_target="tpu_custom_call" | custom-call | tf_op jit(solution)/shard_map/output_gather/pallas_call | solution.py:509
  348.3 1.4 convert_element_type.100
  349.7 1.5 slice_bitcast_fusion
  (93 shorter events, 34.0 us)
Async XLA Ops:
  1.6 4.5 %collective-permute-start = (f32[1024,32]{0,1:T(8,128)S(1)}, f32[1024,32]{0,1:T(8,128)S(1)}, u32[]{:S(2)}, u32[]{:S(2)}) collective-permute-start(f32[1024,32]{0,1:T(8,128)S(1)} %constant_dynamic-slice_fusion.1), channel_id=1, source_target_pairs={{0,1},{1,0},{2,3},{3,2},{4,5},{5,4},{6,7},{7,6},{8,9},{9,8},{10,11... | collective-permute-start | bytes 393224 | tf_op jit(solution)/shard_map/ppermute | solution.py:539
  2.9 4.2 %collective-permute-start.1 = (bf16[1024,384]{1,0:T(8,128)(2,1)S(1)}, bf16[1024,384]{1,0:T(8,128)(2,1)}, u32[]{:S(2)}, u32[]{:S(2)}) collective-permute-start(bf16[1024,384]{1,0:T(8,128)(2,1)S(1)} %constant_dynamic-slice_fusion), channel_id=1, source_target_pairs={{0,1},{1,0},{2,3},{3,2},{4,5},{5,4},{6,7},{7,6},{8,9},{9,8},{10,11... | collective-permute-start | bytes 2359304 | tf_op jit(solution)/shard_map/ppermute | solution.py:539
  96.7 33.0 %copy-start = (f32[64,1024]{1,0:T(8,128)S(1)}, f32[64,1024]{1,0:T(8,128)}, u32[]{:S(2)}) copy-start(f32[64,1024]{1,0:T(8,128)} %small_totals.4) | copy-start | bytes 786436
  114.0 17.4 %copy-start.2 = (f32[64,1024]{1,0:T(8,128)S(1)}, f32[64,1024]{1,0:T(8,128)}, u32[]{:S(2)}) copy-start(f32[64,1024]{1,0:T(8,128)} %small_totals.5) | copy-start | bytes 786436
  214.7 17.3 %copy-start.1 = (f32[64,1024]{1,0:T(8,128)S(1)}, f32[64,1024]{1,0:T(8,128)}, u32[]{:S(2)}) copy-start(f32[64,1024]{1,0:T(8,128)} %small_totals.6) | copy-start | bytes 786436

commit v2 on v0

v2 whole, which is shorter than its diff:
```python
import functools

import jax
import jax.numpy as jnp
from jax import lax
from jax.experimental import pallas as pl
from jax.experimental.pallas import tpu as pltpu
from jax.sharding import PartitionSpec as P

ITERS = 3
MESH = pl.DeviceIdType.MESH
RIDGE = 1.0
EARLY = 2
LATE = 2
SLOT_BYTES = 40 << 20


def dot_t(left, right):
    return lax.dot_general(
        left,
        right,
        (((1,), (1,)), ((), ())),
        precision=lax.Precision.HIGHEST,
        preferred_element_type=jnp.float32,
    )


def dot_h(left, right):
    return jnp.dot(
        left, right, precision=lax.Precision.HIGHEST, preferred_element_type=jnp.float32
    )


def columns(index, width):
    return pl.ds(pl.multiple_of(index * width, 128), width)


def partner(me, step, n):
    bit, total = 1, 0
    while bit < n:
        total = total + (me // bit + step // bit) % 2 * bit
        bit *= 2
    return total


def loop(start, stop, body):
    def step(i, carry):
        body(i)
        return carry

    lax.fori_loop(start, stop, step, 0)


def parts_of(values):
    upper = values.astype(jnp.bfloat16)
    lower = (values - upper.astype(jnp.float32)).astype(jnp.bfloat16)
    return jnp.concatenate([upper, lower], axis=0)


def in_parts(values, right, contract):
    rows = values.shape[0]
    both = lax.dot_general(
        parts_of(values), right, (((1,), (contract,)), ((), ())),
        preferred_element_type=jnp.float32,
    )
    return both[:rows] + both[rows:]


def inverse_of(gram):
    size = gram.shape[0]
    rows = lax.broadcasted_iota(jnp.int32, (size, 2 * size), 0)
    lanes = lax.broadcasted_iota(jnp.int32, (size, 2 * size), 1)
    unit = (lanes == rows + size).astype(jnp.float32)
    work = jnp.concatenate([gram, jnp.zeros_like(gram)], axis=1) + unit
    for k in range(size):
        pivot = work[k : k + 1, :] / work[k : k + 1, k : k + 1]
        work = jnp.where(rows == k, pivot, work - work[:, k : k + 1] * pivot)
    return work[:, size:]


def solve_kernel(
    n_samp, n_rhs, n_feat,
    right_ref, basis, shrink_ref, design, sol_out, res_out,
    slots, narrow, acc, part, up, cross, images, give, side, side_in, chip, chip_in, own,
    sent, direction, applied, residual, projected, back_ref, sol, rest, rest_in,
    g_send, g_held, g_mine, g_across, g_out, f_send, f_held, f_mine, f_across, f_out,
    load_sem, out_sem, piece_send, piece_recv, twin_send, twin_recv,
    up_send, up_recv, cross_recv, down_send, down_recv,
    side_send, side_recv, chip_send, chip_recv, rest_send, rest_recv,
    g_sems, gz_sems, f_sems, fz_sems,
):
    samp, core = lax.axis_index("samples"), lax.axis_index("rhs")
    feat = lax.axis_index("features")
    n = n_samp * n_rhs
    me = samp * n_rhs + core
    count, width, chunk = part.shape
    held = slots.shape[0]
    spare = count - held
    piece = right_ref.shape[1]
    share = width // n_rhs
    half = n_feat // 2
    low = feat < half
    inner = jnp.logical_or(feat == half - 1, feat == half)
    outer = jnp.logical_not(inner)
    is_end = jnp.logical_or(feat == 0, feat == n_feat - 1)
    has_prev = jnp.logical_not(is_end)
    following = jnp.where(low, feat + 1, feat - 1)
    before = jnp.where(low, feat - 1, feat + 1)
    f32, bf16 = jnp.float32, jnp.bfloat16

    def place(index):
        return {"samples": lax.div(index, n_rhs), "rhs": lax.rem(index, n_rhs)}

    def chip_of(step):
        return partner(samp, step, n_samp)

    def core_of(step):
        return partner(core, step, n_rhs)

    def cols(chip_index, core_index):
        return columns(chip_index * n_rhs + core_index, piece)

    def remote(src, dst, send, recv, where):
        return pltpu.make_async_remote_copy(
            src_ref=src, dst_ref=dst, send_sem=send, recv_sem=recv,
            device_id=where, device_id_type=MESH,
        )

    def load(place_in_all):
        slot = lax.rem(place_in_all, held)
        row = pl.multiple_of(lax.rem(place_in_all, count) * chunk, chunk)
        return pltpu.make_async_copy(
            design.at[pl.ds(row, chunk), :], slots.at[slot], load_sem.at[slot]
        )

    loop(0, held, lambda c: load(c).start())

    barrier = pltpu.get_barrier_semaphore()
    for step in range(1, n):
        pl.semaphore_signal(
            barrier, inc=1, device_id=place(lax.rem(me + step, n)), device_id_type=MESH
        )
    for step in range(1, n_feat):
        pl.semaphore_signal(
            barrier, inc=1, device_id={"features": lax.rem(feat + step, n_feat)},
            device_id_type=MESH,
        )
    pl.semaphore_wait(barrier, n - 1 + n_feat - 1)

    def totals(send, held_in, mine, across, out, sems, z_sems):
        def scatter(step):
            peer = lax.rem(me + step, n)
            return remote(
                send.at[peer], held_in.at[me], sems.at[0, step], sems.at[1, step], place(peer)
            )

        def along(step):
            peer = lax.rem(feat + step, n_feat)
            return remote(
                mine, across.at[feat], z_sems.at[0, step], z_sems.at[1, step], {"features": peer}
            )

        def gather(step):
            peer = lax.rem(me + step, n)
            return remote(
                out.at[me], out.at[me], sems.at[2, step], sems.at[3, step], place(peer)
            )

        def first():
            for step in range(1, n):
                scatter(step).start()

        def second():
            total = send[me].astype(f32)
            for step in range(1, n):
                scatter(step).wait_recv()
            for step in range(1, n):
                total = total + held_in[lax.rem(me + step, n)].astype(f32)
            mine[...] = total.astype(mine.dtype)
            for step in range(1, n_feat):
                along(step).start()
            across[feat] = total.astype(mine.dtype)

        def third():
            for step in range(1, n_feat):
                along(step).wait_recv()
            total = across[0].astype(f32)
            for index in range(1, n_feat):
                total = total + across[index].astype(f32)
            out[me] = total.astype(out.dtype)
            for step in range(1, n):
                gather(step).start()

        def fourth():
            for step in range(1, n):
                gather(step).wait_recv()

        def end():
            for step in range(1, n):
                scatter(step).wait_send()
                gather(step).wait_send()
            for step in range(1, n_feat):
                along(step).wait_send()

        return first, second, third, fourth, end

    g_first, g_second, g_third, g_fourth, g_end = totals(
        g_send, g_held, g_mine, g_across, g_out, g_sems, gz_sems
    )
    f_first, f_second, f_third, f_fourth, f_end = totals(
        f_send, f_held, f_mine, f_across, f_out, f_sems, fz_sems
    )
    f_rows, f_lanes = f_send.shape[1:]
    g_rows = g_send.shape[1]

    def factor_inner(values):
        inner_product = jnp.dot(values, basis[...], preferred_element_type=f32)
        for s in range(n_samp):
            for c in range(n_rhs):
                block = inner_product[s * f_rows : (s + 1) * f_rows, c * f_lanes : (c + 1) * f_lanes]
                f_send[s * n_rhs + c] = block.astype(bf16)

    def factor_total():
        lines = []
        for s in range(n_samp):
            line = [f_out[s * n_rhs + c].astype(f32) for c in range(n_rhs)]
            lines.append(jnp.concatenate(line, axis=1))
        return jnp.concatenate(lines, axis=0)

    def piece_copy(step, side_of):
        return remote(
            sent, narrow.at[side_of, :, cols(samp, core)], piece_send.at[step],
            piece_recv.at[step], {"samples": chip_of(step)},
        )

    def twin_copy(step, other, side_of):
        block = narrow.at[side_of, :, cols(chip_of(step), core)]
        return remote(
            block, block, twin_send.at[step, other], twin_recv.at[step, other],
            {"rhs": core_of(other)},
        )

    def give_out(values, side_of):
        sent[...] = values.astype(bf16)
        for step in range(1, n_samp):
            piece_copy(step, side_of).start()
        narrow[side_of, :, cols(samp, core)] = values.astype(bf16)

    def take_in(side_of, use):
        def arrive(step):
            @pl.when(step > 0)
            def _():
                piece_copy(step, side_of).wait_recv()

            for other in range(1, n_rhs):
                twin_copy(step, other, side_of).start()

            def by_core(other):
                @pl.when(other > 0)
                def _():
                    twin_copy(step, other, side_of).wait_recv()

                if use is not None:
                    use(cols(chip_of(step), core_of(other)))

            loop(0, n_rhs, by_core)

        loop(0, n_samp, arrive)

    def end_pieces(side_of):
        for step in range(1, n_samp):
            piece_copy(step, side_of).wait_send()
        for step in range(n_samp):
            for other in range(1, n_rhs):
                twin_copy(step, other, side_of).wait_send()

    def up_copy(c):
        return remote(
            give.at[c], up.at[c], up_send.at[c], up_recv.at[c], {"features": following}
        )

    def cross_copy(c):
        return remote(
            give.at[c], cross.at[c], up_send.at[c], cross_recv.at[c], {"features": following}
        )

    def down_copy(c):
        return remote(
            images.at[c], images.at[c], down_send.at[c], down_recv.at[c], {"features": before}
        )

    def pass_up(c):
        @pl.when(inner)
        def _():
            cross_copy(c).start()

        @pl.when(outer)
        def _():
            up_copy(c).start()

    def up_first(c):
        @pl.when(is_end)
        def _():
            give[c] = part[c].astype(bf16)
            pass_up(c)

    def up_step(c):
        @pl.when(has_prev)
        def _():
            up_copy(c).wait_recv()
            total = part[c] + up[c].astype(f32)
            part[c] = total
            give[c] = total.astype(bf16)
            pass_up(c)

    def cross_step(c):
        @pl.when(inner)
        def _():
            cross_copy(c).wait_recv()
            images[c] = (part[c] + cross[c].astype(f32)).astype(bf16)

            @pl.when(has_prev)
            def _():
                down_copy(c).start()

    def ready(c):
        @pl.when(outer)
        def _():
            down_copy(c).wait_recv()

            @pl.when(has_prev)
            def _():
                down_copy(c).start()

    def side_copy(step, other):
        return remote(
            side.at[step, other - 1], side_in.at[step, other - 1],
            side_send.at[step, other], side_recv.at[step, other], {"rhs": core_of(other)},
        )

    def chip_copy(step):
        return remote(
            chip.at[step], chip_in.at[step], chip_send.at[step], chip_recv.at[step],
            {"samples": chip_of(step)},
        )

    def chip_total(step):
        total = own[...]
        for other in range(1, n_rhs):
            side_copy(step, other).wait_recv()
            total = total + side_in[step, other - 1].astype(f32)
        return total

    def operate(turn, side_of):
        base = turn * spare

        def slot_of(c):
            return lax.rem(base + c, held)

        acc[...] = jnp.zeros_like(acc)
        for c in range(EARLY):
            part[c] = jnp.zeros((width, chunk), f32)

        @pl.when(turn == 0)
        def _():
            for c in range(EARLY):
                load(c).wait()

        def first_terms(place_cols):
            for c in range(EARLY):
                part[c] = part[c] + lax.dot_general(
                    narrow[side_of, :, place_cols], slots[slot_of(c), :, place_cols],
                    (((1,), (1,)), ((), ())), preferred_element_type=f32,
                )

        take_in(side_of, first_terms)

        def rest_copy(step):
            peer = lax.rem(me + step, n)
            row = pl.multiple_of(lax.rem(peer, n_rhs) * share, 16)
            return remote(
                rest.at[pl.ds(row, share), :], rest_in.at[:, columns(me, piece)],
                rest_send.at[step], rest_recv.at[step], place(peer),
            )

        @pl.when(turn == ITERS - 1)
        def _():
            rest[...] = residual[...].astype(bf16)
            for step in range(1, n):
                rest_copy(step).start()
            rest_in[:, columns(me, piece)] = rest[pl.ds(pl.multiple_of(core * share, 16), share), :]

        for c in range(EARLY):
            up_first(c)

        def image_step(c):
            @pl.when(jnp.logical_or(turn == 0, c >= held))
            def _():
                load(base + c).wait()

            part[c] = lax.dot_general(
                narrow[side_of], slots[slot_of(c)],
                (((1,), (1,)), ((), ())), preferred_element_type=f32,
            )
            up_first(c)
            loop(jnp.where(c == EARLY, 0, c - 1), c, up_step)
            loop(
                jnp.where(c <= EARLY + 1, 0, c - 2), jnp.where(c == EARLY, 0, c - 1), cross_step
            )

        def feature_step(c):
            ready(c)
            acc[...] = acc[...] + jnp.dot(
                images[c], slots[slot_of(c)], preferred_element_type=f32
            )

            @pl.when(c + held < count)
            def _():
                load(base + c + held).start()

        middle = spare + max((held - LATE) // 2 - 1, 0)

        def both_steps(part_of):
            loop(
                jnp.where(part_of == 0, EARLY, held), jnp.where(part_of == 0, held, count),
                image_step,
            )

            def step(c):
                feature_step(c)

                @pl.when(jnp.logical_and(part_of == 1, c == middle))
                def _():
                    up_step(count - 1)
                    cross_step(count - 2)

            loop(
                jnp.where(part_of == 0, 0, spare), jnp.where(part_of == 0, spare, count - LATE),
                step,
            )

        loop(0, 2, both_steps)
        cross_step(count - 1)
        for c in range(count - LATE, count):
            ready(c)

        def piece_total(place_cols):
            total = acc[:, place_cols]
            for c in range(count - LATE, count):
                total = total + jnp.dot(
                    images[c], slots[slot_of(c), :, place_cols], preferred_element_type=f32
                )
            return total

        def leave(i):
            step = n_samp - 1 - i

            def by_core(j):
                other = n_rhs - 1 - j
                total = piece_total(cols(chip_of(step), core_of(other)))

                @pl.when(other > 0)
                def _():
                    side[step, jnp.maximum(other - 1, 0)] = total.astype(bf16)
                    side_copy(step, jnp.maximum(other, 1)).start()

                @pl.when(jnp.logical_and(j == 0, step < n_samp - 1))
                def _():
                    chip[step + 1] = chip_total(step + 1).astype(bf16)
                    chip_copy(step + 1).start()

                @pl.when(other == 0)
                def _():
                    own[...] = total

            loop(0, n_rhs, by_core)

        loop(0, n_samp, leave)
        total = chip_total(0)
        for step in range(n_samp - 1, 0, -1):
            chip_copy(step).wait_recv()
            total = total + chip_in[step].astype(f32)
        applied[...] = total + RIDGE * direction[...]

        end_pieces(side_of)
        for step in range(1, n_samp):
            chip_copy(step).wait_send()
        for step in range(n_samp):
            for other in range(1, n_rhs):
                side_copy(step, other).wait_send()

        def end_chunk(c):
            up_copy(c).wait_send()

            @pl.when(has_prev)
            def _():
                down_copy(c).wait_send()

        loop(0, count, end_chunk)

        @pl.when(turn == ITERS - 1)
        def _():
            for step in range(1, n):
                rest_copy(step).wait_send()
                rest_copy(step).wait_recv()

    shrink = shrink_ref[...]
    factor_inner(right_ref[...].astype(bf16))
    f_first()
    residual[...] = right_ref[...]
    sol[...] = jnp.zeros_like(sol)
    f_second()
    f_third()
    f_fourth()
    projected[...] = factor_total()
    f_end()
    direction[...] = residual[...] + in_parts(shrink * projected[...], basis[...], 1)

    def iteration(turn):
        side_of = lax.rem(turn, 2)
        last = turn == ITERS - 1
        more = turn < ITERS - 1
        give_out(direction[...], side_of)
        operate(turn, side_of)
        block = dot_t(
            jnp.concatenate([direction[...], applied[...]], axis=0),
            jnp.concatenate([applied[...], residual[...]], axis=0),
        )
        for index in range(n):
            g_send[index] = block[index * g_rows : (index + 1) * g_rows]
        g_first()

        @pl.when(more)
        def _():
            factor_inner(applied[...].astype(bf16))
            f_first()

        @pl.when(last)
        def _():
            give_out(applied[...], 1 - side_of)

        g_second()

        @pl.when(more)
        def _():
            f_second()

        g_third()

        @pl.when(more)
        def _():
            f_third()

        @pl.when(last)
        def _():
            take_in(1 - side_of, None)

        g_fourth()
        summed = g_out[...].reshape(2 * width, 2 * width)
        g_end()
        gram = summed[:width, :width]
        inverse = inverse_of(0.5 * (gram + gram.T))
        back = dot_h(inverse, summed[:width, width:])
        back_t = back.T
        back_ref[...] = back_t
        mine = back_ref[pl.ds(pl.multiple_of(core * share, 8), share), :]
        sol[...] = sol[...] + in_parts(mine, narrow[side_of], 0)

        @pl.when(more)
        def _():
            left = residual[...] - dot_h(back_t, applied[...])
            residual[...] = left
            f_fourth()
            factor_image = factor_total()
            f_end()
            projection = projected[...] - dot_h(back_t, factor_image)
            projected[...] = projection
            scaled = left + in_parts(shrink * projection, basis[...], 1)
            image_new = summed[width:, width:] - dot_h(summed[width:, :width], back)
            image_new = image_new + dot_t(factor_image, shrink * projection)
            next_t = dot_h(inverse, image_new).T
            direction[...] = scaled - dot_h(next_t, direction[...])

        @pl.when(last)
        def _():
            acc[:share, :] = rest_in[...].astype(f32) - in_parts(mine, narrow[1 - side_of], 0)
            end_pieces(1 - side_of)

    loop(0, ITERS, iteration)
    first_out = pltpu.make_async_copy(sol, sol_out, out_sem.at[0])
    second_out = pltpu.make_async_copy(acc.at[pl.ds(0, share), :], res_out, out_sem.at[1])
    first_out.start()
    second_out.start()
    first_out.wait()
    second_out.wait()


def solve(n_samp, n_rhs, n_feat, right, basis, shrink, design):
    width, piece = right.shape
    rows, feats = design.shape
    rank = basis.shape[1]
    n = n_samp * n_rhs
    chunk = min(512, rows // 4)
    count = rows // chunk
    held = min(count, SLOT_BYTES // (chunk * feats * 2))
    share = width // n_rhs
    wide = (width, piece)
    blocks = (count, width, chunk)
    g_part = (2 * width // n, 2 * width)
    f_part = (width // n_samp, rank // n_rhs)
    vmem, dma = pltpu.VMEM, pltpu.SemaphoreType.DMA
    bf16, f32 = jnp.bfloat16, jnp.float32
    in_vmem, anywhere = pl.BlockSpec(memory_space=vmem), pl.BlockSpec(memory_space=pl.ANY)
    return pl.pallas_call(
        functools.partial(solve_kernel, n_samp, n_rhs, n_feat),
        name="solve",
        out_shape=[jax.ShapeDtypeStruct((share, feats), f32)] * 2,
        in_specs=[in_vmem, in_vmem, in_vmem, anywhere],
        out_specs=[anywhere, anywhere],
        scratch_shapes=[
            vmem((held, chunk, feats), bf16), vmem((2, width, feats), bf16),
            vmem((width, feats), f32),
            vmem(blocks, f32), vmem(blocks, bf16), vmem(blocks, bf16), vmem(blocks, bf16),
            vmem(blocks, bf16),
            vmem((n_samp, n_rhs - 1) + wide, bf16), vmem((n_samp, n_rhs - 1) + wide, bf16),
            vmem((n_samp,) + wide, bf16), vmem((n_samp,) + wide, bf16), vmem(wide, f32),
            vmem(wide, bf16), vmem(wide, f32), vmem(wide, f32), vmem(wide, f32),
            vmem((width, rank), f32), vmem((width, width), f32), vmem((share, feats), f32),
            vmem(wide, bf16), vmem((share, feats), bf16),
            vmem((n,) + g_part, f32), vmem((n,) + g_part, f32), vmem(g_part, f32),
            vmem((n_feat,) + g_part, f32), vmem((n,) + g_part, f32),
            vmem((n,) + f_part, bf16), vmem((n,) + f_part, bf16), vmem(f_part, bf16),
            vmem((n_feat,) + f_part, bf16), vmem((n,) + f_part, bf16),
            dma((held,)), dma((2,)), dma((n_samp,)), dma((n_samp,)),
            dma((n_samp, n_rhs)), dma((n_samp, n_rhs)),
            dma((count,)), dma((count,)), dma((count,)), dma((count,)), dma((count,)),
            dma((n_samp, n_rhs)), dma((n_samp, n_rhs)), dma((n_samp,)), dma((n_samp,)),
            dma((n,)), dma((n,)),
            dma((4, n)), dma((2, n_feat)), dma((4, n)), dma((2, n_feat)),
        ],
        compiler_params=pltpu.CompilerParams(
            collective_id=1, has_side_effects=True, vmem_limit_bytes=62 << 20
        ),
    )(right, basis, shrink, design)


def shards(n_samp, n_feat, n_rhs, design, right_side, factor, nystrom_values):
    feat_rows = right_side.shape[0]
    n = n_samp * n_rhs
    piece = feat_rows // n
    samp, rhs = lax.axis_index("samples"), lax.axis_index("rhs")
    shrink = (1.0 + jnp.min(nystrom_values)) / (1.0 + nystrom_values) - 1.0

    def own_rows(block):
        def rows_for(core):
            return lax.dynamic_slice_in_dim(block, (samp * n_rhs + core) * piece, piece, 0)

        parts = [None] * n_rhs
        moved = [rows_for(rhs)]
        for step in range(1, n_rhs):
            pairs = [(i, (i + step) % n_rhs) for i in range(n_rhs)]
            moved.append(lax.ppermute(rows_for((rhs + step) % n_rhs), "rhs", pairs))
        for core in range(n_rhs):
            best = moved[0]
            for step in range(1, n_rhs):
                best = jnp.where((rhs - step) % n_rhs == core, moved[step], best)
            parts[core] = best
        return jnp.concatenate(parts, axis=1)

    basis = own_rows(factor)
    residual = own_rows(right_side).T
    sol, res = solve(n_samp, n_rhs, n_feat, residual, basis, shrink[None, :], design)
    return sol.T, res.T


def solution(mesh):
    placed = (P(("samples", "rhs"), "features"), P("features", "rhs"), P("features", "rhs"), P())
    sizes = (mesh.shape["samples"], mesh.shape["features"], mesh.shape["rhs"])
    return jax.shard_map(
        functools.partial(shards, *sizes),
        mesh=mesh,
        in_specs=placed,
        out_specs=(P("features", "rhs"), P("features", "rhs")),
        check_vma=False,
    )
```

time: 523 us -> 264 us (0.50)
  matrix products: 183 us -> 0 us
  other arithmetic: 53.2 us -> 6.36 us
  Pallas kernels: 275 us -> 247 us
    dot_general x39 -> x0, matrix products: 182 us -> none  [the longest x3 85.1 us: shards(): lax.dot_general(narrow, design, (((1,), (1,)), ((), ())), preferred_eleme...]
    another operation x15 -> x0, other arithmetic: 36.2 us -> none  [the longest x9 19.6 us: shards(): chol_lower = jnp.linalg.cholesky(gram)]
    pallas_call x14 -> x1, Pallas kernels: 275 us -> 247 us  [solve(): pl.pallas_call(functools.partial(solve_kernel, n_samp, n_rhs, n_feat), na...]
    convert_element_type x12 -> x0, other arithmetic: 6.11 us -> none  [the longest x4 2.93 us: parts_of(): upper = values.astype(jnp.bfloat16)]
  transfers between devices with their start and end apart: 2 -> 2, of which waited for: 0 -> 0; matrix products, arithmetic and copies ran while one was open for 1% -> 2% of each run, Pallas kernels for 0% -> 0%
where the time goes in v2:
time: 264 us; the launch traced here: 263 us
  Pallas kernels  247 us (94%)
  local copies, waits for them, and re-layouts  7.25 us (3%)
  other arithmetic  6.36 us (2%)
    pallas_call x1, Pallas kernels, solve(): pl.pallas_call(functools.partial(solve_kernel, n_samp, n_rhs, n_feat), na...  247 us
  transfers between devices with their start and end apart: 2, of which 0 were waited for; matrix products, arithmetic and copies ran while one was open for 2% of the time, Pallas kernels for 0%

profile of v2, /device:TPU:1, one launch (start us, length us, event | category | flops | bytes accessed | tf_op | source)
XLA Modules:
  0.0 262.8 jit_solution(3885807959176611836)
XLA Ops:
  0.6 1.2 constant_dynamic-slice_fusion
  1.9 0.1 collective-permute-start.1
  2.0 0.9 constant_dynamic-slice_fusion.1
  2.9 0.6 collective-permute-start
  3.4 1.3 reduce_min.9
  5.4 0.7 divide_add_fusion
  6.1 0.6 broadcast_in_dim.3.shrink_ref
  6.7 0.0 collective-permute-done
  6.7 0.9 dynamic-slice_select_fusion.1
  7.6 0.7 maximum_bitcast_fusion.right_ref
  8.3 0.0 collective-permute-done.1
  8.3 1.4 broadcast_select_fusion.1
  9.7 1.3 pad_maximum_fusion.basis
  11.0 247.2 %solve.1 = (f32[32,8192]{1,0:T(8,128)}, f32[32,8192]{1,0:T(8,128)}) custom-call(f32[64,1024]{1,0:T(8,128)} %maximum_bitcast_fusion.right_ref, bf16[1024,768]{1,0:T(8,128)(2,1)} %pad_maximum_fusion.basis, f32[1,768]{1,0:T(1,128)} %broadcast_in_dim.3.shrink_ref, bf16[4096,8192]{1,0:T(8,128)(2,1)} %design.1), custom_call_target="tpu_custom_call" | custom-call | tf_op jit(solution)/shard_map/solve/pallas_call | solution.py:614
  258.2 2.3 copy.8
  260.5 2.3 copy.9
Async XLA Ops:
  1.9 6.4 %collective-permute-start.1 = (bf16[1024,384]{1,0:T(8,128)(2,1)S(1)}, bf16[1024,384]{1,0:T(8,128)(2,1)S(1)}, u32[]{:S(2)}, u32[]{:S(2)}) collective-permute-start(bf16[1024,384]{1,0:T(8,128)(2,1)S(1)} %constant_dynamic-slice_fusion), channel_id=1, source_target_pairs={{0,1},{1,0},{2,3},{3,2},{4,5},{5,4},{6,7},{7,6},{8,9},{9,8},{10,11... | collective-permute-start | bytes 2359304 | tf_op jit(solution)/shard_map/ppermute | solution.py:662
  2.9 3.8 %collective-permute-start = (f32[1024,32]{0,1:T(8,128)S(1)}, f32[1024,32]{0,1:T(8,128)S(1)}, u32[]{:S(2)}, u32[]{:S(2)}) collective-permute-start(f32[1024,32]{0,1:T(8,128)S(1)} %constant_dynamic-slice_fusion.1), channel_id=1, source_target_pairs={{0,1},{1,0},{2,3},{3,2},{4,5},{5,4},{6,7},{7,6},{8,9},{9,8},{10,11... | collective-permute-start | bytes 393224 | tf_op jit(solution)/shard_map/ppermute | solution.py:662

commit v3 on v2

--- a/solution.py
+++ b/solution.py
@@ -10,7 +10,7 @@
 ITERS = 3
 MESH = pl.DeviceIdType.MESH
 RIDGE = 1.0
-EARLY = 2
+EARLY = 3
 LATE = 2
 SLOT_BYTES = 40 << 20
 
@@ -80,23 +80,24 @@
 
 def solve_kernel(
     n_samp, n_rhs, n_feat,
-    right_ref, basis, shrink_ref, design, sol_out, res_out,
-    slots, narrow, acc, part, up, cross, images, give, side, side_in, chip, chip_in, own,
+    right_ref, factor, values_ref, design, sol_out, res_out,
+    basis, slots, narrow, acc, part, up, cross, images, give, side, side_in, chip, chip_in,
     sent, direction, applied, residual, projected, back_ref, sol, rest, rest_in,
     g_send, g_held, g_mine, g_across, g_out, f_send, f_held, f_mine, f_across, f_out,
     load_sem, out_sem, piece_send, piece_recv, twin_send, twin_recv,
     up_send, up_recv, cross_recv, down_send, down_recv,
     side_send, side_recv, chip_send, chip_recv, rest_send, rest_recv,
-    g_sems, gz_sems, f_sems, fz_sems,
+    g_sems, gz_sems, f_sems, fz_sems, basis_sems,
 ):
     samp, core = lax.axis_index("samples"), lax.axis_index("rhs")
     feat = lax.axis_index("features")
     n = n_samp * n_rhs
     me = samp * n_rhs + core
-    count, width, chunk = part.shape
+    count, width, chunk = images.shape
+    ring = part.shape[0]
     held = slots.shape[0]
     spare = count - held
-    piece = right_ref.shape[1]
+    piece = residual.shape[1]
     share = width // n_rhs
     half = n_feat // 2
     low = feat < half
@@ -126,14 +127,24 @@
             device_id=where, device_id_type=MESH,
         )
 
-    def load(place_in_all):
-        slot = lax.rem(place_in_all, held)
-        row = pl.multiple_of(lax.rem(place_in_all, count) * chunk, chunk)
+    def slot_of(turn, c):
+        return lax.rem(turn * spare + c, held)
+
+    def load(turn, c, slot):
+        later = spare + lax.rem(c - spare + held + spare * turn, held)
+        row = pl.multiple_of(jnp.where(c < spare, c, later) * chunk, chunk)
         return pltpu.make_async_copy(
             design.at[pl.ds(row, chunk), :], slots.at[slot], load_sem.at[slot]
         )
 
-    loop(0, held, lambda c: load(c).start())
+    def load_first(turn, c):
+        return load(turn, c, slot_of(turn, c))
+
+    def load_again(turn, c):
+        return load(turn, c, slot_of(turn, c + spare))
+
+    right_copy = pltpu.make_async_copy(right_ref, residual, out_sem.at[0])
+    right_copy.start()
 
     barrier = pltpu.get_barrier_semaphore()
     for step in range(1, n):
@@ -146,6 +157,26 @@
             device_id_type=MESH,
         )
     pl.semaphore_wait(barrier, n - 1 + n_feat - 1)
+
+    lanes = factor.shape[1]
+
+    def factor_rows(core_index):
+        return factor.at[pl.ds(pl.multiple_of((samp * n_rhs + core_index) * piece, 16), piece), :]
+
+    factor_own = pltpu.make_async_copy(
+        factor_rows(core), basis.at[:, columns(core, lanes)], basis_sems.at[0, 0]
+    )
+
+    def factor_copy(other):
+        return remote(
+            factor_rows(core_of(other)), basis.at[:, columns(core, lanes)],
+            basis_sems.at[0, other], basis_sems.at[1, other], {"rhs": core_of(other)},
+        )
+
+    for other in range(1, n_rhs):
+        factor_copy(other).start()
+    factor_own.start()
+    loop(0, held, lambda c: load_first(0, c).start())
 
     def totals(send, held_in, mine, across, out, sems, z_sems):
         def scatter(step):
@@ -301,15 +332,15 @@
     def up_first(c):
         @pl.when(is_end)
         def _():
-            give[c] = part[c].astype(bf16)
+            give[c] = part[lax.rem(c, ring)].astype(bf16)
             pass_up(c)
 
     def up_step(c):
         @pl.when(has_prev)
         def _():
             up_copy(c).wait_recv()
-            total = part[c] + up[c].astype(f32)
-            part[c] = total
+            total = part[lax.rem(c, ring)] + up[c].astype(f32)
+            part[lax.rem(c, ring)] = total
             give[c] = total.astype(bf16)
             pass_up(c)
 
@@ -317,7 +348,7 @@
         @pl.when(inner)
         def _():
             cross_copy(c).wait_recv()
-            images[c] = (part[c] + cross[c].astype(f32)).astype(bf16)
+            images[c] = (part[lax.rem(c, ring)] + cross[c].astype(f32)).astype(bf16)
 
             @pl.when(has_prev)
             def _():
@@ -340,36 +371,31 @@
 
     def chip_copy(step):
         return remote(
-            chip.at[step], chip_in.at[step], chip_send.at[step], chip_recv.at[step],
+            chip.at[step - 1], chip_in.at[step - 1], chip_send.at[step], chip_recv.at[step],
             {"samples": chip_of(step)},
         )
 
     def chip_total(step):
-        total = own[...]
+        total = applied[...]
         for other in range(1, n_rhs):
             side_copy(step, other).wait_recv()
             total = total + side_in[step, other - 1].astype(f32)
         return total
 
     def operate(turn, side_of):
-        base = turn * spare
-
-        def slot_of(c):
-            return lax.rem(base + c, held)
-
         acc[...] = jnp.zeros_like(acc)
         for c in range(EARLY):
-            part[c] = jnp.zeros((width, chunk), f32)
+            part[lax.rem(c, ring)] = jnp.zeros((width, chunk), f32)
 
         @pl.when(turn == 0)
         def _():
             for c in range(EARLY):
-                load(c).wait()
+                load_first(turn, c).wait()
 
         def first_terms(place_cols):
             for c in range(EARLY):
-                part[c] = part[c] + lax.dot_general(
-                    narrow[side_of, :, place_cols], slots[slot_of(c), :, place_cols],
+                part[lax.rem(c, ring)] = part[lax.rem(c, ring)] + lax.dot_general(
+                    narrow[side_of, :, place_cols], slots[slot_of(turn, c), :, place_cols],
                     (((1,), (1,)), ((), ())), preferred_element_type=f32,
                 )
 
@@ -392,55 +418,61 @@
 
         for c in range(EARLY):
             up_first(c)
+            if c < spare:
+                load_first(turn, c + held).start()
+
+        def summed_by(c):
+            return jnp.where(c > EARLY, c, jnp.where(c == EARLY, 1, 0))
 
         def image_step(c):
             @pl.when(jnp.logical_or(turn == 0, c >= held))
             def _():
-                load(base + c).wait()
-
-            part[c] = lax.dot_general(
-                narrow[side_of], slots[slot_of(c)],
+                load_first(turn, c).wait()
+
+            part[lax.rem(c, ring)] = lax.dot_general(
+                narrow[side_of], slots[slot_of(turn, c)],
                 (((1,), (1,)), ((), ())), preferred_element_type=f32,
             )
             up_first(c)
-            loop(jnp.where(c == EARLY, 0, c - 1), c, up_step)
-            loop(
-                jnp.where(c <= EARLY + 1, 0, c - 2), jnp.where(c == EARLY, 0, c - 1), cross_step
-            )
-
-        def feature_step(c):
+
+            @pl.when(c < spare)
+            def _():
+                load_first(turn, c + held).start()
+
+            loop(summed_by(c - 1), summed_by(c), up_step)
+            loop(summed_by(c - 2), summed_by(c - 1), cross_step)
+
+        loop(EARLY, count, image_step)
+        kept = count - LATE - spare
+
+        def feature_step(i):
+            c = jnp.where(i < kept, spare + i, i - kept)
+            again = c < spare
+
+            @pl.when(again)
+            def _():
+                load_again(turn, c).wait()
+
             ready(c)
             acc[...] = acc[...] + jnp.dot(
-                images[c], slots[slot_of(c)], preferred_element_type=f32
+                images[c], slots[slot_of(turn, jnp.where(again, c + spare, c))],
+                preferred_element_type=f32,
             )
 
-            @pl.when(c + held < count)
-            def _():
-                load(base + c + held).start()
-
-        middle = spare + max((held - LATE) // 2 - 1, 0)
-
-        def both_steps(part_of):
-            loop(
-                jnp.where(part_of == 0, EARLY, held), jnp.where(part_of == 0, held, count),
-                image_step,
-            )
-
-            def step(c):
-                feature_step(c)
-
-                @pl.when(jnp.logical_and(part_of == 1, c == middle))
-                def _():
-                    up_step(count - 1)
-                    cross_step(count - 2)
-
-            loop(
-                jnp.where(part_of == 0, 0, spare), jnp.where(part_of == 0, spare, count - LATE),
-                step,
-            )
-
-        loop(0, 2, both_steps)
-        cross_step(count - 1)
+            @pl.when(i < spare)
+            def _():
+                load_again(turn, i).start()
+
+            @pl.when(i == 1)
+            def _():
+                up_step(count - 1)
+                cross_step(count - 2)
+
+            @pl.when(i == 3)
+            def _():
+                cross_step(count - 1)
+
+        loop(0, count - LATE, feature_step)
         for c in range(count - LATE, count):
             ready(c)
 
@@ -448,7 +480,7 @@
             total = acc[:, place_cols]
             for c in range(count - LATE, count):
                 total = total + jnp.dot(
-                    images[c], slots[slot_of(c), :, place_cols], preferred_element_type=f32
+                    images[c], slots[slot_of(turn, c), :, place_cols], preferred_element_type=f32
                 )
             return total
 
@@ -466,12 +498,12 @@
 
                 @pl.when(jnp.logical_and(j == 0, step < n_samp - 1))
                 def _():
-                    chip[step + 1] = chip_total(step + 1).astype(bf16)
+                    chip[step] = chip_total(step + 1).astype(bf16)
                     chip_copy(step + 1).start()
 
                 @pl.when(other == 0)
                 def _():
-                    own[...] = total
+                    applied[...] = total
 
             loop(0, n_rhs, by_core)
 
@@ -479,7 +511,7 @@
         total = chip_total(0)
         for step in range(n_samp - 1, 0, -1):
             chip_copy(step).wait_recv()
-            total = total + chip_in[step].astype(f32)
+            total = total + chip_in[step - 1].astype(f32)
         applied[...] = total + RIDGE * direction[...]
 
         end_pieces(side_of)
@@ -504,10 +536,14 @@
                 rest_copy(step).wait_send()
                 rest_copy(step).wait_recv()
 
-    shrink = shrink_ref[...]
-    factor_inner(right_ref[...].astype(bf16))
+    values = values_ref[...]
+    shrink = (1.0 + jnp.min(values, axis=1, keepdims=True)) / (1.0 + values) - 1.0
+    right_copy.wait()
+    factor_own.wait()
+    for other in range(1, n_rhs):
+        factor_copy(other).wait()
+    factor_inner(residual[...].astype(bf16))
     f_first()
-    residual[...] = right_ref[...]
     sol[...] = jnp.zeros_like(sol)
     f_second()
     f_third()
@@ -595,10 +631,10 @@
     second_out.wait()
 
 
-def solve(n_samp, n_rhs, n_feat, right, basis, shrink, design):
+def solve(n_samp, n_rhs, n_feat, right, factor, values, design):
     width, piece = right.shape
     rows, feats = design.shape
-    rank = basis.shape[1]
+    rank = values.shape[1]
     n = n_samp * n_rhs
     chunk = min(512, rows // 4)
     count = rows // chunk
@@ -615,15 +651,16 @@
         functools.partial(solve_kernel, n_samp, n_rhs, n_feat),
         name="solve",
         out_shape=[jax.ShapeDtypeStruct((share, feats), f32)] * 2,
-        in_specs=[in_vmem, in_vmem, in_vmem, anywhere],
+        in_specs=[anywhere, anywhere, in_vmem, anywhere],
         out_specs=[anywhere, anywhere],
         scratch_shapes=[
+            vmem((piece, rank), bf16),
             vmem((held, chunk, feats), bf16), vmem((2, width, feats), bf16),
             vmem((width, feats), f32),
-            vmem(blocks, f32), vmem(blocks, bf16), vmem(blocks, bf16), vmem(blocks, bf16),
+            vmem((min(count, 6), width, chunk), f32), vmem(blocks, bf16), vmem(blocks, bf16), vmem(blocks, bf16),
             vmem(blocks, bf16),
             vmem((n_samp, n_rhs - 1) + wide, bf16), vmem((n_samp, n_rhs - 1) + wide, bf16),
-            vmem((n_samp,) + wide, bf16), vmem((n_samp,) + wide, bf16), vmem(wide, f32),
+            vmem((n_samp - 1,) + wide, bf16), vmem((n_samp - 1,) + wide, bf16),
             vmem(wide, bf16), vmem(wide, f32), vmem(wide, f32), vmem(wide, f32),
             vmem((width, rank), f32), vmem((width, width), f32), vmem((share, feats), f32),
             vmem(wide, bf16), vmem((share, feats), bf16),
@@ -636,12 +673,12 @@
             dma((count,)), dma((count,)), dma((count,)), dma((count,)), dma((count,)),
             dma((n_samp, n_rhs)), dma((n_samp, n_rhs)), dma((n_samp,)), dma((n_samp,)),
             dma((n,)), dma((n,)),
-            dma((4, n)), dma((2, n_feat)), dma((4, n)), dma((2, n_feat)),
+            dma((4, n)), dma((2, n_feat)), dma((4, n)), dma((2, n_feat)), dma((2, n_rhs)),
         ],
         compiler_params=pltpu.CompilerParams(
             collective_id=1, has_side_effects=True, vmem_limit_bytes=62 << 20
         ),
-    )(right, basis, shrink, design)
+    )(right, factor, values, design)
 
 
 def shards(n_samp, n_feat, n_rhs, design, right_side, factor, nystrom_values):
@@ -649,7 +686,6 @@
     n = n_samp * n_rhs
     piece = feat_rows // n
     samp, rhs = lax.axis_index("samples"), lax.axis_index("rhs")
-    shrink = (1.0 + jnp.min(nystrom_values)) / (1.0 + nystrom_values) - 1.0
 
     def own_rows(block):
         def rows_for(core):
@@ -667,9 +703,8 @@
             parts[core] = best
         return jnp.concatenate(parts, axis=1)
 
-    basis = own_rows(factor)
     residual = own_rows(right_side).T
-    sol, res = solve(n_samp, n_rhs, n_feat, residual, basis, shrink[None, :], design)
+    sol, res = solve(n_samp, n_rhs, n_feat, residual, factor, nystrom_values[None, :], design)
     return sol.T, res.T
 
 

time: 264 us -> 244 us (0.924)
  Pallas kernels: 247 us -> 233 us
  other arithmetic: 6.36 us -> 1.65 us
    pallas_call x1, Pallas kernels: 247 us -> 233 us  [solve(): pl.pallas_call(functools.partial(solve_kernel, n_samp, n_rhs, n_feat), na...]
  transfers between devices with their start and end apart: 2 -> 1, of which waited for: 0 -> 0; matrix products, arithmetic and copies ran while one was open for 2% -> 1% of each run, Pallas kernels for 0% -> 0%
where the time goes in v3:
time: 244 us; the launch traced here: 243 us
  Pallas kernels  233 us (95%)
  local copies, waits for them, and re-layouts  6.71 us (3%)
    pallas_call x1, Pallas kernels, solve(): pl.pallas_call(functools.partial(solve_kernel, n_samp, n_rhs, n_feat), na...  233 us
  transfers between devices with their start and end apart: 1, of which 0 were waited for; matrix products, arithmetic and copies ran while one was open for 1% of the time, Pallas kernels for 0%

profile of v3, /device:TPU:1, one launch (start us, length us, event | category | flops | bytes accessed | tf_op | source)
XLA Modules:
  0.0 242.6 jit_solution(12932090625156593682)
XLA Ops:
  0.6 0.9 constant_dynamic-slice_fusion
  1.6 0.1 collective-permute-start
  1.7 1.3 broadcast_in_dim.3.values_ref
  2.9 0.0 collective-permute-done
  3.0 0.9 dynamic-slice_select_fusion.1
  3.9 0.7 maximum_bitcast_fusion.right_ref
  4.6 233.4 %solve.1 = (f32[32,8192]{1,0:T(8,128)}, f32[32,8192]{1,0:T(8,128)}) custom-call(f32[64,1024]{1,0:T(8,128)} %maximum_bitcast_fusion.right_ref, bf16[8192,384]{1,0:T(8,128)(2,1)} %factor.1, f32[1,768]{1,0:T(1,128)} %broadcast_in_dim.3.values_ref, bf16[4096,8192]{1,0:T(8,128)(2,1)} %design.1), custom_call_target="tpu_custom_call" | custom-call | tf_op jit(solution)/shard_map/solve/pallas_call | solution.py:650
  238.0 2.3 copy.8
  240.3 2.3 copy.9
Async XLA Ops:
  1.6 1.4 collective-permute-start
